TPU v7x, 32 devices: a whole 2x2x4 slice. The times are simulated.
32 devices in a mesh: sky: 8 (over z, y), band: 4 (over x, core).
Axes of the slice: x: 2, y: 2, z: 4, core: 2. Of those that a mesh axis runs over, the one named last changes fastest.
Arguments:
- magnitudes: float32 [4, 8, 16384], P('band', None, 'sky'), may hold values from -7 to 7
- weights: float32 [4, 8, 16384], P('band', None, 'sky'), may hold values from 0.25 to 4
- slots: int32 [4, 8, 16384], P('band', None, 'sky'), may hold values from 0 to 31, as said below
- block_fields: int32 [64, 32], P('sky'), may hold values from 0 to 4096, as said below
- owner: int32 [4096], replicated, may hold values from 0 to 7, as said below
- colors: int32 [4096], replicated, may hold values from 0 to 7
- color_terms: float32 [4, 4], replicated, may hold values from -0.25 to 0.25
Outputs:
- zero_points: float32 [4, 4096], P('band', 'sky')
- star_mags: float32 [4, 16384], P('band', 'sky')
- misfit: float32 [4, 4], P(None, 'band')
Inputs may be any that keep to these rules, and one draw needn't show every extreme that they name: `block_fields`: the live entries of each list come first, are distinct, and name fields owned by the block's own sky tile or by the tiles one index below or above it, cyclically over 8 tiles; the remaining entries equal 4096. A list holds 16 or more live entries, and every tile has a block with all 32 live. `owner`: each sky tile owns exactly 512 fields. `slots`: each observation names a live entry of its block's list.
All inputs are finite; a program needn't handle non-finite values.
Results may differ from a plain program's by a relative error of at most 0.00023.
Values sent between devices are 32-bit elements; how exact they have to be, the bound alone decides.
A program may use at most 64 MiB of HBM per device.

v0:
```python
import jax
import jax.numpy as jnp
from jax import lax
from jax.sharding import PartitionSpec as P

COLORS = 8
SWEEPS = 4


PRIOR_WEIGHT = 1.0


def from_behind(value, axis, steps):
    count = lax.axis_size(axis)
    pairs = [(source, (source + steps) % count) for source in range(count)]
    return lax.ppermute(value, axis, pairs)


def body(magnitudes, weights, slots, block_fields, owner, colors, color_terms):
    band_count = color_terms.shape[0]
    tiles = lax.axis_size("sky")
    my_tile = lax.axis_index("sky")
    my_band = lax.axis_index("band")
    band_mags, band_wts, band_slots = (magnitudes, weights, slots)
    own_row = 0
    band_rows, obs_count, star_count = band_mags.shape
    block_count, list_len = block_fields.shape
    block_rows = star_count // block_count
    fields = owner.shape[0]
    slot_grid = band_slots.reshape(band_rows, obs_count, block_count, block_rows)
    entries = jnp.arange(list_len, dtype=jnp.int32)
    star_weight = jnp.sum(band_wts, axis=1)
    mixing = (
        jnp.eye(band_count, dtype=jnp.float32)
        + color_terms
        - jnp.diag(jnp.sum(color_terms, axis=1))
    )
    owner_order = jnp.argsort(owner, stable=True)
    owned = fields // tiles

    def slot_sums(values):
        grid = values.reshape(band_rows, obs_count, block_count, block_rows)
        hits = slot_grid[..., None] == entries
        return jnp.sum(jnp.where(hits, grid[..., None], 0.0), axis=(1, 3))

    def spread(list_vals):
        hits = slot_grid[..., None] == entries
        picked = jnp.sum(jnp.where(hits, list_vals[:, None, :, None, :], 0.0), axis=4)
        return picked.reshape(band_rows, obs_count, star_count)

    def predict(zp_obs):
        star_means = jnp.sum(band_wts * (band_mags - zp_obs), axis=1) / star_weight
        all_means = lax.all_gather(star_means, "band", axis=0, tiled=True)
        mix_row = lax.dynamic_index_in_dim(mixing, my_band, 0, keepdims=True)
        predicted = jnp.dot(mix_row, all_means, precision=lax.Precision.HIGHEST)
        return (star_means, predicted)

    positions = jnp.argsort(owner_order, stable=True)
    rank_in = positions - owner * owned
    live = block_fields < fields
    safe_ids = jnp.minimum(block_fields, fields - 1)
    relative = jnp.mod(jnp.take(owner, safe_ids) - my_tile + 1, tiles)
    list_ids = jnp.where(live, relative * owned + jnp.take(rank_in, safe_ids), 3 * owned)
    segments = 3 * owned
    nearby_idx = jnp.mod(my_tile + jnp.arange(3, dtype=jnp.int32) - 1, tiles)
    near_fields = jnp.take(owner_order.reshape(tiles, owned), nearby_idx, axis=0)
    zp_colors = jnp.take(colors, near_fields)[None]
    zero_pts = jnp.zeros((band_rows, 3, owned), jnp.float32)

    def flatten(table):
        return table.reshape(band_rows, 3 * owned)

    def combine(partial_flat):
        partial_sums = partial_flat.reshape(band_rows, 3, owned)
        from_left = from_behind(partial_sums[:, 1:3], "sky", 1)
        from_right = from_behind(partial_sums[:, 0:2], "sky", -1)
        far_left = from_behind(partial_sums[:, 2], "sky", 2)
        far_right = from_behind(partial_sums[:, 0], "sky", -2)
        below = far_left + from_left[:, 0] + partial_sums[:, 0]
        middle = from_left[:, 1] + partial_sums[:, 1] + from_right[:, 0]
        above = partial_sums[:, 2] + from_right[:, 1] + far_right
        return jnp.stack([below, middle, above], axis=1)

    def lookup(table):
        padded = jnp.concatenate([flatten(table), jnp.zeros((band_rows, 1), jnp.float32)], axis=1)
        return spread(jnp.take(padded, list_ids, axis=1))

    def segment_band(per_band):
        return jax.ops.segment_sum(
            per_band.reshape(-1), list_ids.reshape(-1), num_segments=segments + 1
        )[:segments]

    def totals(values):
        per_slot = slot_sums(values)
        return combine(jax.vmap(segment_band)(per_slot))

    denominators = totals(band_wts) + PRIOR_WEIGHT

    def squared_misfit(residual, zp_obs):
        per_band = jnp.sum(band_wts * (residual - zp_obs) ** 2, axis=(1, 2))
        return lax.dynamic_index_in_dim(per_band, own_row, 0, keepdims=False)

    def advance(table, color_no):
        zp_obs = lookup(table)
        star_means, predicted = predict(zp_obs)
        residual = band_mags - predicted[:, None, :]
        updated = totals(band_wts * residual) / denominators
        local_value = squared_misfit(residual, zp_obs)
        return (jnp.where(zp_colors == color_no, updated, table), local_value)

    def later_colors(color_no, table):
        return advance(table, color_no)[0]

    def record(local_value):
        return lax.psum(local_value, "sky")

    recorded = []
    for sweep_no in range(SWEEPS):
        zero_pts, local_value = advance(zero_pts, 0)
        if sweep_no > 0:
            recorded.append(record(local_value))
        zero_pts = lax.fori_loop(1, COLORS, later_colors, zero_pts)
    zp_obs = lookup(zero_pts)
    star_means, predicted = predict(zp_obs)
    residual = band_mags - predicted[:, None, :]
    recorded.append(record(squared_misfit(residual, zp_obs)))
    stacked = jnp.stack(recorded)
    misfit = stacked / (obs_count * star_count * tiles)
    own_zp = lax.dynamic_index_in_dim(zero_pts[:, 1], own_row, 0, keepdims=True)
    own_means = lax.dynamic_index_in_dim(star_means, own_row, 0, keepdims=True)
    return (own_zp, own_means, misfit[:, None])


def solution(mesh):
    in_specs = (
        P("band", None, "sky"),
        P("band", None, "sky"),
        P("band", None, "sky"),
        P("sky", None),
        P(),
        P(),
        P(),
    )
    out_specs = (P("band", "sky"), P("band", "sky"), P(None, "band"))
    return jax.shard_map(body, mesh=mesh, in_specs=in_specs, out_specs=out_specs, check_vma=False)
```

profile of v0, /device:TPU:0, one launch (start us, length us, event | category | flops | bytes accessed | tf_op | source)
XLA Modules:
  0.0 838.3 jit_solution(8149706508148525772)
XLA Ops:
  0.7 6.5 sort.31
  7.2 5.8 sort.32
  20.3 6.2 all-gather.4
  42.8 8.4 gather_fusion.5
  60.7 166.6 %while.68 = (s32[]{:T(128)}, f32[1,3,512]{2,1,0:T(4,128)S(1)}, s32[1,3,512]{2,1,0:T(4,128)S(1)}, s32[8,32]{1,0:T(8,128)S(1)}, s32[1,8,2048]{2,1,0:T(8,128)S(1)},...) while((s32[]{:T(128)}, f32[1,3,512]{2,1,0:T(4,128)S(1)}, ...), condition=%wide.wide.region_15.18_spmd.clone, body=%wide.wide.region_10.17_spmd.clone.sunk | while | flops 3325443 | bytes 1340753 | solution.py:122
  63.3 5.2 all-gather.21
  86.7 5.2 all-gather.21
  111.2 5.2 all-gather.21
  134.4 5.2 all-gather.21
  159.0 5.2 all-gather.21
  182.2 5.2 all-gather.21
  206.7 5.2 all-gather.21
  229.8 5.2 all-gather.5
  249.6 170.6 %while.69 = (s32[]{:T(128)}, f32[1,3,512]{2,1,0:T(4,128)S(1)}, s32[1,3,512]{2,1,0:T(4,128)S(1)}, s32[8,32]{1,0:T(8,128)S(1)}, s32[1,8,2048]{2,1,0:T(8,128)S(1)},...) while((s32[]{:T(128)}, f32[1,3,512]{2,1,0:T(4,128)S(1)}, ...), condition=%wide.wide.region_25.28_spmd.clone, body=%wide.wide.region_20.27_spmd.clone.sunk | while | flops 3325443 | bytes 1471825 | solution.py:122
  252.3 5.2 all-gather.22
  279.6 5.2 all-gather.22
  302.7 5.2 all-gather.22
  327.4 5.2 all-gather.22
  350.5 5.2 all-gather.22
  375.1 5.2 all-gather.22
  398.2 5.2 all-gather.22
  422.7 5.4 all-gather.6
  442.8 170.6 %while.70 = (s32[]{:T(128)}, f32[1,3,512]{2,1,0:T(4,128)S(1)}, s32[1,3,512]{2,1,0:T(4,128)S(1)}, s32[8,32]{1,0:T(8,128)S(1)}, s32[1,8,2048]{2,1,0:T(8,128)S(1)},...) while((s32[]{:T(128)}, f32[1,3,512]{2,1,0:T(4,128)S(1)}, ...), condition=%wide.wide.region_35.38_spmd.clone, body=%wide.wide.region_30.37_spmd.clone.sunk | while | flops 3325443 | bytes 1471825 | solution.py:122
  445.5 5.2 all-gather.23
  472.8 5.2 all-gather.23
  495.9 5.2 all-gather.23
  520.6 5.2 all-gather.23
  543.7 5.2 all-gather.23
  568.3 5.2 all-gather.23
  635.8 170.8 %while.71 = (s32[]{:T(128)}, f32[1,3,512]{2,1,0:T(4,128)S(1)}, s32[1,3,512]{2,1,0:T(4,128)S(1)}, s32[8,32]{1,0:T(8,128)S(1)}, s32[1,8,2048]{2,1,0:T(8,128)S(1)},...) while((s32[]{:T(128)}, f32[1,3,512]{2,1,0:T(4,128)S(1)}, ...), condition=%wide.wide.region_45.48_spmd.clone, body=%wide.wide.region_40.47_spmd.clone.sunk | while | flops 3325443 | bytes 1471825 | solution.py:122
  810.4 5.2 all-gather.8
  816.5 18.4 %all-reduce = (f32[1,1]{0,1:T(1,128)}, f32[1,1]{0,1:T(1,128)}, f32[1,1]{0,1:T(1,128)}, f32[1,1]{0,1:T(1,128)}) all-reduce(f32[1,1]{0,1:T(1,128)} %bitcast.70, f32[1,1]{0,1:T(1,128)} %bitcast.66, f32[1,1]{0,1:T(1,128)} %bitcast.65, f32[1,1]{0,1:T(1,128)} %bitcast.64), channel_id=1, replica_groups=mesh['sky'=8,'band'=4] {'sky'}, use_global_device_ids=true, to_apply=%region_55.58 | all-reduce | flops 4 | bytes 32 | tf_op jit(solution)/shard_map/psum | solution.py:115
  (1206 shorter events, 667.1 us)
Async XLA Ops:
  29.9 21.3 %collective-permute-start.21 = (f32[1,2,512]{2,1,0:T(2,128)S(1)}, f32[1,2,512]{2,1,0:T(2,128)S(1)}, u32[]{:S(2)}, u32[]{:S(2)}) collective-permute-start(f32[1,2,512]{2,1,0:T(2,128)S(1)} %get-tuple-element.1354), channel_id=1, source_target_pairs={{0,4},{4,8},{8,12},{12,16},{16,20},{20,24},{24,28},{28,0},{1,5},{5... | collective-permute-start | bytes 12296 | tf_op jit(solution)/shard_map/ppermute | solution.py:16
  31.9 19.4 %collective-permute-start.22 = (f32[1,2,512]{2,1,0:T(2,128)S(1)}, f32[1,2,512]{2,1,0:T(2,128)S(1)}, u32[]{:S(2)}, u32[]{:S(2)}) collective-permute-start(f32[1,2,512]{2,1,0:T(2,128)S(1)} %get-tuple-element.1355), channel_id=1, source_target_pairs={{0,28},{4,0},{8,4},{12,8},{16,12},{20,16},{24,20},{28,24},{1,29},{... | collective-permute-start | bytes 12296 | tf_op jit(solution)/shard_map/ppermute | solution.py:16
  37.2 17.9 %collective-permute-start.17 = (f32[1,2,512]{2,1,0:T(2,128)S(1)}, f32[1,2,512]{2,1,0:T(2,128)S(1)}, u32[]{:S(2)}, u32[]{:S(2)}) collective-permute-start(f32[1,2,512]{2,1,0:T(2,128)S(1)} %get-tuple-element.1361), channel_id=1, source_target_pairs={{0,4},{4,8},{8,12},{12,16},{16,20},{20,24},{24,28},{28,0},{1,5},{5... | collective-permute-start | bytes 12296 | tf_op jit(solution)/shard_map/ppermute | solution.py:16
  37.3 17.8 %collective-permute-start.18 = (f32[1,2,512]{2,1,0:T(2,128)S(1)}, f32[1,2,512]{2,1,0:T(2,128)S(1)}, u32[]{:S(2)}, u32[]{:S(2)}) collective-permute-start(f32[1,2,512]{2,1,0:T(2,128)S(1)} %get-tuple-element.1362), channel_id=1, source_target_pairs={{0,28},{4,0},{8,4},{12,8},{16,12},{20,16},{24,20},{28,24},{1,29},{... | collective-permute-start | bytes 12296 | tf_op jit(solution)/shard_map/ppermute | solution.py:16
  51.2 7.9 collective-permute-start.20
  51.3 7.9 collective-permute-start.23
  72.2 6.3 collective-permute-start.1
  96.8 6.3 collective-permute-start.1
  120.0 6.3 collective-permute-start.1
  144.5 6.3 collective-permute-start.1
  167.7 6.3 collective-permute-start.1
  192.3 6.3 collective-permute-start.1
  215.5 6.3 collective-permute-start.1
  237.8 6.4 collective-permute-start.25
  265.2 6.3 collective-permute-start.5
  288.3 6.3 collective-permute-start.5
  312.9 6.3 collective-permute-start.5
  336.0 6.3 collective-permute-start.5
  360.7 6.3 collective-permute-start.5
  383.8 6.3 collective-permute-start.5
  431.0 6.4 collective-permute-start.29
  458.4 6.3 collective-permute-start.9
  481.5 6.3 collective-permute-start.9
  577.0 6.3 collective-permute-start.9
  601.6 6.3 collective-permute-start.9
  624.0 6.4 collective-permute-start.33
  646.5 6.4 collective-permute-start.12
  651.6 6.3 collective-permute-start.13
  674.7 6.3 collective-permute-start.13
  699.4 6.3 collective-permute-start.13
  722.5 6.3 collective-permute-start.13
  747.1 6.3 collective-permute-start.13
  (108 other events, 589.1 us)
where the time goes:
time: 846 us; the launch traced here: 838 us
  starting transfers between devices  220 us (26%)
  waiting for transfers between devices  212 us (25%)
  blocking collectives  191 us (23%)
  other arithmetic  120 us (14%)
  local copies, waits for them, and re-layouts  82.9 us (10%)
    ppermute x132, starting transfers between devices, from_behind(): return lax.ppermute(value, axis, pairs)  220 us
    ppermute x132, waiting for transfers between devices, from_behind(): return lax.ppermute(value, axis, pairs)  212 us
    all_gather x33, blocking collectives, predict(): all_means = lax.all_gather(star_means, 'band', axis=0, tiled=True)  172 us
    scatter-add x33, other arithmetic, segment_band(): jax.ops.segment_sum(per_band.reshape(-1), list_ids.reshape(-1), num_segme...  67.8 us
    gather x66, local copies, waits for them, and re-layouts, lookup(): return spread(jnp.take(padded, list_ids, axis=1))  59.3 us
    psum x1, blocking collectives, record(): return lax.psum(local_value, 'sky')  18.4 us
    reduce_sum x33, other arithmetic, spread(): jnp.sum(jnp.where(hits, list_vals[:, None, :, None, :], 0.0), axis=4)  18.2 us
  transfers between devices with their start and end apart: 132, of which 91 were waited for; matrix products, arithmetic and copies ran while one was open for 1% of the time, Pallas kernels for 0%

commit v1 on v0

v1 whole, which is shorter than its diff:
```python
import functools

import jax
import jax.numpy as jnp
from jax import lax
from jax.experimental import pallas as pl
from jax.experimental.pallas import tpu as pltpu
from jax.sharding import PartitionSpec as P

COLORS = 8
SWEEPS = 4
PRIOR_WEIGHT = 1.0
REACH = 2
HIGHEST = lax.Precision.HIGHEST
LANES = 128
EXTRA = 8


def contract_lanes(left, right):
    dims = (((1,), (1,)), ((), ()))
    return lax.dot_general(left, right, dims, precision=HIGHEST, preferred_element_type=jnp.float32)


def couple_kernel(bands, obs, list_len, rows, mix_ref, mix_grid_ref, data_ref, out_ref):
    blocks = out_ref.shape[0]
    entry = lax.broadcasted_iota(jnp.int32, (list_len, rows), 0).astype(jnp.float32)
    for block in range(blocks):
        cols = pl.ds(block * rows, rows)
        one_hot, one_hot_mag, star_weight, means = [], [], [], []
        for band in range(bands):
            mags = data_ref[band, 0:obs, cols]
            wts = data_ref[band, obs : 2 * obs, cols]
            slots = data_ref[band, 2 * obs : 3 * obs, cols]
            scaled = wts * mags
            weight_sum = jnp.sum(wts, axis=0, keepdims=True)
            star_weight.append(weight_sum)
            means.append(jnp.sum(scaled, axis=0, keepdims=True) / weight_sum)
            hot = jnp.zeros((list_len, rows), jnp.float32)
            hot_mag = jnp.zeros((list_len, rows), jnp.float32)
            for k in range(obs):
                hit = slots[k : k + 1] == entry
                hot = hot + jnp.where(hit, wts[k : k + 1], 0.0)
                hot_mag = hot_mag + jnp.where(hit, scaled[k : k + 1], 0.0)
            one_hot.append(hot)
            one_hot_mag.append(hot_mag)
        rest = []
        shares = []
        for band in range(bands):
            predicted = mix_ref[band, 0] * means[0]
            for other in range(1, bands):
                predicted = predicted + mix_ref[band, other] * means[other]
            rest.append(one_hot_mag[band] - one_hot[band] * predicted)
            shares.append(one_hot[band] / star_weight[band])
        hot_all = jnp.concatenate(one_hot, axis=0)
        share_all = jnp.concatenate(shares, axis=0)
        rest_all = jnp.concatenate(rest, axis=0)
        out_ref[block, 0:LANES, :] = contract_lanes(share_all, hot_all) * mix_grid_ref[...]
        ones = jnp.ones((8, rows), jnp.float32)
        rest_row = contract_lanes(ones, rest_all)
        weight_row = contract_lanes(ones, hot_all)
        first = lax.broadcasted_iota(jnp.int32, (8, LANES), 0) == 0
        out_ref[block, LANES : LANES + EXTRA, :] = jnp.where(first, rest_row, weight_row)


def sweep_kernel(tiles, blocks, coupled_ref, pick_ref, color_ref, out_ref, kt, base, tot, rden, zp, stage, sems):
    near = 2 * REACH + 1

    def fetch(tile, slot):
        return pltpu.make_async_copy(
            coupled_ref.at[pl.ds(tile * blocks, blocks)], stage.at[slot], sems.at[slot]
        )

    def tile_rows(tile):
        return pl.ds(pl.multiple_of(tile * blocks, blocks), blocks)

    fetch(0, 0).start()

    def unpack(tile, carry):
        slot = lax.rem(tile, 2)

        @pl.when(tile + 1 < tiles)
        def _():
            fetch(tile + 1, 1 - slot).start()

        fetch(tile, slot).wait()
        for block in range(blocks):
            kt[pl.ds(tile * (LANES * blocks) + block, LANES, stride=blocks), :] = stage[slot, block, 0:LANES, :]
            base[pl.ds(tile * blocks + block, 1), :] = stage[slot, block, LANES : LANES + 1, :]
            tot[pl.ds(tile * blocks + block, 1), :] = stage[slot, block, LANES + 1 : LANES + 2, :]
        return carry

    lax.fori_loop(0, tiles, unpack, 0)

    def gathered(tile):
        sums = [jnp.zeros((blocks, LANES), jnp.float32) for _ in range(4)]
        for offset in range(near):
            source = lax.rem(tile + offset + tiles - REACH, tiles) * blocks
            for block in range(blocks):
                place = offset * blocks + block
                pick = pick_ref[tile, place]
                row = jnp.broadcast_to(tot[pl.ds(source + block, 1), :], (blocks, LANES))
                got = jnp.take_along_axis(row, pick & (LANES - 1), axis=1, mode="promise_in_bounds")
                sums[place % 4] = sums[place % 4] + jnp.where(pick < LANES, got, 0.0)
        return (sums[0] + sums[1]) + (sums[2] + sums[3])

    def weigh(tile, carry):
        rden[tile_rows(tile), :] = 1.0 / (gathered(tile) + PRIOR_WEIGHT)
        return carry

    lax.fori_loop(0, tiles, weigh, 0)
    zp[...] = jnp.zeros_like(zp)

    def step(number, carry):
        color_no = lax.rem(number, COLORS)

        def total(tile, inner):
            here = zp[tile_rows(tile), :]
            sums = [base[tile_rows(tile), :]] + [jnp.zeros((blocks, LANES), jnp.float32) for _ in range(3)]
            for j in range(LANES):
                rows = pl.ds(pl.multiple_of(tile * (LANES * blocks) + j * blocks, blocks), blocks)
                value = jnp.broadcast_to(here[:, j : j + 1], (blocks, LANES))
                sums[j % 4] = sums[j % 4] + value * kt[rows, :]
            tot[tile_rows(tile), :] = (sums[0] + sums[1]) + (sums[2] + sums[3])
            return inner

        lax.fori_loop(0, tiles, total, 0, unroll=2)

        def update(tile, inner):
            rows = tile_rows(tile)
            fresh = gathered(tile) * rden[rows, :]
            zp[rows, :] = jnp.where(color_ref[rows, :] == color_no, fresh, zp[rows, :])
            return inner

        lax.fori_loop(0, tiles, update, 0, unroll=2)

        @pl.when(color_no == COLORS - 1)
        def _():
            out_ref[lax.div(number, COLORS)] = zp[...]

        return carry

    lax.fori_loop(0, SWEEPS * COLORS, step, 0)


def finish_kernel(bands, obs, list_len, rows, mix_ref, data_ref, own_ref, zp_two_ref, zp_own_ref, means_ref, misfit_ref):
    my_band = lax.axis_index("band")
    halves = rows // LANES

    def spread(row, picks):
        table = jnp.broadcast_to(row, (obs, LANES))
        return jnp.take_along_axis(table, picks, axis=1, mode="promise_in_bounds")

    for block in range(zp_own_ref.shape[0]):
        row = zp_own_ref[block : block + 1, :]
        for half in range(halves):
            cols = pl.ds(block * rows + half * LANES, LANES)
            wts = own_ref[obs : 2 * obs, cols]
            picks = own_ref[2 * obs : 3 * obs, cols].astype(jnp.int32) + my_band * list_len
            left = wts * (own_ref[0:obs, cols] - spread(row, picks))
            means_ref[0:1, cols] = jnp.sum(left, axis=0, keepdims=True) / jnp.sum(wts, axis=0, keepdims=True)

    for sweep in range(SWEEPS):
        partial = [jnp.zeros((obs, LANES), jnp.float32) for _ in range(bands)]
        for block in range(zp_two_ref.shape[1]):
            row = zp_two_ref[sweep, block : block + 1, :]
            for half in range(halves):
                cols = pl.ds(block * rows + half * LANES, LANES)
                left, means = [], []
                for band in range(bands):
                    wts = data_ref[band, obs : 2 * obs, cols]
                    picks = data_ref[band, 2 * obs : 3 * obs, cols].astype(jnp.int32) + band * list_len
                    mags = data_ref[band, 0:obs, cols] - spread(row, picks)
                    left.append(mags)
                    means.append(jnp.sum(wts * mags, axis=0, keepdims=True) / jnp.sum(wts, axis=0, keepdims=True))
                for band in range(bands):
                    predicted = mix_ref[band, 0] * means[0]
                    for other in range(1, bands):
                        predicted = predicted + mix_ref[band, other] * means[other]
                    wts = data_ref[band, obs : 2 * obs, cols]
                    partial[band] = partial[band] + wts * (left[band] - predicted) ** 2
        for band in range(bands):
            line = jnp.sum(partial[band], axis=0, keepdims=True)
            misfit_ref[sweep * bands + band : sweep * bands + band + 1, :] = line


def body(magnitudes, weights, slots, block_fields, owner, colors, color_terms):
    bands = color_terms.shape[0]
    tiles = lax.axis_size("sky")
    my_tile = lax.axis_index("sky")
    my_band = lax.axis_index("band")
    _, obs, stars = magnitudes.shape
    blocks, list_len = block_fields.shape
    rows = stars // blocks
    fields = owner.shape[0]
    owned = fields // tiles
    mine = blocks // bands
    mixing = (
        jnp.eye(bands, dtype=jnp.float32) + color_terms - jnp.diag(jnp.sum(color_terms, axis=1))
    )
    vmem = pl.BlockSpec(memory_space=pltpu.VMEM)
    smem = pl.BlockSpec(memory_space=pltpu.SMEM)
    hbm = pl.BlockSpec(memory_space=pl.ANY)

    own = jnp.concatenate([magnitudes[0], weights[0], slots[0].astype(jnp.float32)], axis=0)
    data = lax.all_to_all(own, "band", split_axis=1, concat_axis=0, tiled=True)
    data = data.reshape(bands, 3 * obs, mine * rows)
    all_fields = lax.all_gather(block_fields, "sky", axis=0, tiled=True)

    mix_grid = jnp.repeat(jnp.repeat(mixing.T, list_len, axis=0), list_len, axis=1)
    coupled = pl.pallas_call(
        functools.partial(couple_kernel, bands, obs, list_len, rows),
        out_shape=jax.ShapeDtypeStruct((mine, LANES + EXTRA, LANES), jnp.float32),
        in_specs=[smem, vmem, vmem],
        out_specs=vmem,
        name="couple",
    )(mixing, mix_grid, data)
    coupled = lax.all_gather(coupled, ("sky", "band"), axis=0, tiled=True)

    live = all_fields < fields
    entry_colors = jnp.where(live, jnp.take(colors, jnp.minimum(all_fields, fields - 1)), -1)
    entry_colors = jnp.tile(entry_colors, (1, bands))
    by_tile = all_fields.reshape(tiles, blocks, list_len)
    near = jnp.stack([jnp.roll(by_tile, REACH - n, axis=0) for n in range(2 * REACH + 1)], axis=1)
    near = near.reshape(tiles, (2 * REACH + 1) * blocks, list_len)
    lane_fields = jnp.tile(by_tile, (1, 1, bands))[:, None]
    lane_band = jnp.arange(LANES, dtype=jnp.int32) // list_len * list_len
    pick = jnp.full((tiles, near.shape[1], blocks, LANES), LANES, jnp.int32)
    for entry in range(list_len):
        pick = jnp.where(near[:, :, entry][:, :, None, None] == lane_fields, lane_band + entry, pick)
    pick = jnp.where(lane_fields < fields, pick, LANES)

    total_blocks = tiles * blocks
    big = (total_blocks, LANES)
    snapshots = pl.pallas_call(
        functools.partial(sweep_kernel, tiles, blocks),
        out_shape=jax.ShapeDtypeStruct((SWEEPS,) + big, jnp.float32),
        in_specs=[hbm, vmem, vmem],
        out_specs=vmem,
        scratch_shapes=[
            pltpu.VMEM((total_blocks * LANES, LANES), jnp.float32),
            pltpu.VMEM(big, jnp.float32),
            pltpu.VMEM(big, jnp.float32),
            pltpu.VMEM(big, jnp.float32),
            pltpu.VMEM(big, jnp.float32),
            pltpu.VMEM((2, blocks, LANES + EXTRA, LANES), jnp.float32),
            pltpu.SemaphoreType.DMA((2,)),
        ],
        compiler_params=pltpu.CompilerParams(vmem_limit_bytes=60 * 1024 * 1024),
        name="sweeps",
    )(coupled, pick, entry_colors)

    first = my_tile * blocks
    zp_tile = lax.dynamic_slice_in_dim(snapshots[SWEEPS - 1], first, blocks, axis=0)
    zp_two = lax.dynamic_slice_in_dim(snapshots, first + my_band * mine, mine, axis=1)
    star_means, partial = pl.pallas_call(
        functools.partial(finish_kernel, bands, obs, list_len, rows),
        out_shape=(
            jax.ShapeDtypeStruct((1, stars), jnp.float32),
            jax.ShapeDtypeStruct((SWEEPS * bands, LANES), jnp.float32),
        ),
        in_specs=[smem, vmem, vmem, vmem, vmem],
        out_specs=(vmem, vmem),
        name="finish",
    )(mixing, data, own, zp_two, zp_tile)
    partial = jnp.sum(partial, axis=1).reshape(SWEEPS, bands)
    misfit = lax.psum(partial, ("sky", "band")) / (obs * stars * tiles)
    misfit = lax.dynamic_slice_in_dim(misfit, my_band, 1, axis=1)

    tile_ids = jnp.mod(my_tile + jnp.arange(3, dtype=jnp.int32) - 1, tiles)
    close_fields = jnp.concatenate(
        [lax.dynamic_index_in_dim(by_tile, tile_ids[n], 0, keepdims=False) for n in range(3)], axis=0
    ).reshape(-1)
    field_no = jnp.arange(fields, dtype=jnp.int32)[:, None]
    is_mine = (owner == my_tile)[:, None]
    rank = jnp.sum((is_mine & (field_no < close_fields[None])).astype(jnp.int32), axis=0)
    has = jnp.sum((is_mine & (field_no == close_fields[None])).astype(jnp.int32), axis=0) > 0
    rank = jnp.where(has, rank, owned)
    count = close_fields.shape[0]
    entry_no = jnp.arange(count, dtype=jnp.int32)[:, None]
    hit = rank[:, None] == jnp.arange(owned, dtype=jnp.int32)[None]
    chosen = jnp.max(jnp.where(hit, entry_no, -1), axis=0)
    last = lax.dynamic_slice_in_dim(snapshots[SWEEPS - 1], my_band * list_len, list_len, axis=1)
    last = last.reshape(tiles, blocks, list_len)
    close_zp = jnp.concatenate(
        [lax.dynamic_index_in_dim(last, tile_ids[n], 0, keepdims=False) for n in range(3)], axis=0
    ).reshape(-1)
    own_zp = jnp.sum(jnp.where(chosen[None] == entry_no, close_zp[:, None], 0.0), axis=0)
    return own_zp[None], star_means, misfit


def solution(mesh):
    in_specs = (
        P("band", None, "sky"),
        P("band", None, "sky"),
        P("band", None, "sky"),
        P("sky", None),
        P(),
        P(),
        P(),
    )
    out_specs = (P("band", "sky"), P("band", "sky"), P(None, "band"))
    return jax.shard_map(body, mesh=mesh, in_specs=in_specs, out_specs=out_specs, check_vma=False)
```

time: 846 us -> 264 us (0.31)
  starting transfers between devices: 220 us -> 4.24 us
  waiting for transfers between devices: 212 us -> 1.55 us
  blocking collectives: 191 us -> 70.2 us
  Pallas kernels: 0 us -> 118 us
  other arithmetic: 120 us -> 24.2 us
  local copies, waits for them, and re-layouts: 82.9 us -> 24.6 us
  between operations: 1.92 us -> 20.3 us
    ppermute x132 -> x0, starting transfers between devices: 220 us -> none  [from_behind(): return lax.ppermute(value, axis, pairs)]
    ppermute x132 -> x0, waiting for transfers between devices: 212 us -> none  [from_behind(): return lax.ppermute(value, axis, pairs)]
    all_gather x33 -> x1, blocking collectives: 172 us -> 31.7 us  [body(): all_fields = lax.all_gather(block_fields, 'sky', axis=0, tiled=True)]
    pallas_call x0 -> x3, Pallas kernels: none -> 118 us  [the longest x1 113 us: body(): pl.pallas_call(functools.partial(sweep_kernel, tiles, blocks), out_shape=...]
    scatter-add x33 -> x0, other arithmetic: 67.8 us -> none  [segment_band(): jax.ops.segment_sum(per_band.reshape(-1), list_ids.reshape(-1), num_segme...]
    gather x73 -> x2, local copies, waits for them, and re-layouts: 71.9 us -> 11.9 us  [body(): jnp.take(colors, jnp.minimum(all_fields, fields - 1))]
    reduce_sum x99 -> x3, other arithmetic: 32.8 us -> 5.76 us  [the longest x1 4.08 us: body(): jnp.sum((is_mine & (field_no == close_fields[None])).astype(jnp.int32), a...]
    psum x1, blocking collectives: 18.4 us -> 38.5 us  [body(): misfit = lax.psum(partial, ('sky', 'band')) / (obs * stars * tiles)]
  transfers between devices with their start and end apart: 132 -> 2, of which waited for: 91 -> 1; matrix products, arithmetic and copies ran while one was open for 1% -> 15% of each run, Pallas kernels for 0% -> 0%
where the time goes in v1:
time: 264 us; the launch traced here: 263 us
  Pallas kernels  118 us (45%)
  blocking collectives  70.2 us (27%)
  local copies, waits for them, and re-layouts  24.6 us (9%)
  other arithmetic  24.2 us (9%)
  between operations  20.3 us (8%)
  starting transfers between devices  4.24 us (2%)
    pallas_call x1, Pallas kernels, body(): pl.pallas_call(functools.partial(sweep_kernel, tiles, blocks), out_shape=...  113 us
    psum x1, blocking collectives, body(): misfit = lax.psum(partial, ('sky', 'band')) / (obs * stars * tiles)  38.5 us
    all_gather x1, blocking collectives, body(): all_fields = lax.all_gather(block_fields, 'sky', axis=0, tiled=True)  31.7 us
    select_n x1, other arithmetic, body(): pick = jnp.where(lane_fields < fields, pick, LANES)  12 us
    gather x2, local copies, waits for them, and re-layouts, body(): jnp.take(colors, jnp.minimum(all_fields, fields - 1))  11.9 us
    slice x2, local copies, waits for them, and re-layouts, body(): near[:, :, entry][:, :, None, None] == lane_fields  5.82 us
  transfers between devices with their start and end apart: 2, of which 1 were waited for; matrix products, arithmetic and copies ran while one was open for 15% of the time, Pallas kernels for 0%

profile of v1, /device:TPU:0, one launch (start us, length us, event | category | flops | bytes accessed | tf_op | source)
XLA Modules:
  0.0 263.2 jit_solution(2783298847370379067)
XLA Ops:
  7.2 0.9 convert_bitcast_fusion
  8.1 1.6 pad_maximum_fusion
  9.6 4.2 %all-to-all-start = ((f32[24,4,512]{2,0,1:T(8,128)}), f32[24,4,512]{2,0,1:T(8,128)S(1)}, u32[]{:S(2)}, u32[]{:S(2)}) async-start(f32[24,4,512]{2,0,1:T(8,128)} %pad_maximum_fusion), calls=%async_computation | async-start | bytes 393216 | tf_op jit(solution)/shard_map/all_to_all | solution.py:205
  13.9 0.8 reduce_sum.47
  14.7 0.8 fusion.9
  15.5 0.1 reshape.118
  15.6 0.7 copy.28.mix_grid_ref
  16.3 1.3 select_subtract_fusion.mix_ref
  17.6 1.5 all-to-all-done
  19.2 0.7 copy-done.1
  19.8 2.7 %couple.1 = f32[2,136,128]{2,1,0:T(8,128)} custom-call(f32[4,4]{1,0:T(4,128)} %select_subtract_fusion.mix_ref, f32[128,128]{1,0:T(8,128)} %copy.28.mix_grid_ref, f32[4,24,512]{2,1,0:T(8,128)} %bitcast.76), custom_call_target="tpu_custom_call" | custom-call | tf_op jit(solution)/shard_map/couple/pallas_call | solution.py:210
  22.6 0.7 fusion.8
  27.2 31.7 %all_gather.6 = s32[64,32]{1,0:T(8,128)S(1)} all-gather(s32[8,32]{1,0:T(8,128)S(1)} %copy-done.5), channel_id=1, replica_groups=mesh['sky'=8,'band'=4] {'sky'}, dimensions={0}, use_global_device_ids=true | all-gather | bytes 9216 | tf_op jit(solution)/shard_map/all_gather | solution.py:207
  58.9 0.1 tile.17
  59.1 11.8 %gather_fusion = s32[2048]{0:T(1024)S(1)} fusion(s32[4096]{0:T(1024)S(1)} %copy-done, s32[2048]{0:T(1024)S(1)} %broadcast_clamp_fusion), kind=kCustom, calls=%fused_computation | custom fusion | bytes 24576 | tf_op jit(solution)/shard_map/jit(_take)/gather | solution.py:220
  71.1 0.7 copy.31.color_ref
  74.2 2.4 slice_reduce_fusion.30
  76.6 4.1 %convert_reduce_fusion.1 = (s32[768]{0:T(1024)S(1)}, s32[768]{0:T(1024)S(1)}) fusion(s32[768]{0:T(1024)S(1)} %eq.229, pred[4096]{0:T(1024)(128)(4,1)S(1)} %broadcast_compare_fusion.1), kind=kLoop, calls=%fused_computation.3 | loop fusion | flops 25164288 | bytes 13312 | tf_op jit(solution)/shard_map/reduce_sum | solution.py:276
  80.7 0.3 select_reduce_fusion.1
  81.1 3.4 %slice_reduce_fusion.31 = (s32[8,40]{1,0:T(8,128)S(1)}, s32[8,40]{1,0:T(8,128)S(1)}, s32[8,40]{1,0:T(8,128)S(1)}, s32[8,40]{1,0:T(8,128)S(1)}, s32[8,40]{1,0:T(8...) fusion(s32[8,40,32]{2,1,0:T(8,128)S(1)} %bitcast.73), kind=kLoop, calls=%fused_computation.45 | loop fusion | bytes 48640 | tf_op jit(solution)/shard_map/slice | solution.py:229
  84.5 0.7 pad_maximum_fusion.1.own_ref
  85.2 12.0 %select_select_fusion.pick_ref = s32[8,40,8,128]{3,2,1,0:T(8,128)} fusion(s32[128]{0:T(128)S(1)} %get-tuple-element.75, s32[8,40]{1,0:T(8,128)S(1)} %get-tuple-element.23, s32[128]{0:T(128)S(1)} %get-tuple-element.106, s32[8,40]{1,0:T(8,128)S(1)} %get-tuple-element.24, s32[128]{0:T(128)S(1)} %get-tuple-element.76, s32[8,40]{1,0:T(8,128)S(1)} %get-tuple-element.25, ...), kind=kLoop, calls=%fused_computation.11 | loop fusion | flops 21299200 | bytes 1409024 | tf_op jit(solution)/shard_map/jit(_where)/select_n | solution.py:230
  97.2 113.4 %sweeps.1 = f32[4,64,128]{2,1,0:T(8,128)} custom-call(f32[64,136,128]{2,1,0:T(8,128)} %all-gather.2.cloned.1.call-done.coupled_ref, s32[8,40,8,128]{3,2,1,0:T(8,128)} %select_select_fusion.pick_ref, s32[64,128]{1,0:T(8,128)} %copy.31.color_ref), custom_call_target="tpu_custom_call" | custom-call | tf_op jit(solution)/shard_map/sweeps/pallas_call | solution.py:234
  210.6 0.8 slice.262
  211.3 1.3 constant_dynamic-slice_fusion.1.zp_two_ref
  212.7 0.6 dynamic-slice_bitcast_fusion.1.zp_own_ref
  213.2 2.0 finish.1
  215.2 0.8 reduce_sum.49
  216.0 0.1 reshape.122
  216.1 38.5 %psum.7 = f32[4,4]{1,0:T(4,128)S(1)} all-reduce(f32[4,4]{1,0:T(4,128)S(1)} %reshape.122), channel_id=1, replica_groups=mesh['sky'=8,'band'=4] {'sky','band'}, use_global_device_ids=true, to_apply=%region_6.7 | all-reduce | flops 16 | bytes 128 | tf_op jit(solution)/shard_map/psum | solution.py:266
  254.7 0.6 copy.32
  255.5 0.9 select_reduce_fusion
  (62 shorter events, 0.9 us)
Async XLA Ops:
  7.2 52.0 %copy-start = (s32[4096]{0:T(1024)S(1)}, s32[4096]{0:T(1024)}, u32[]{:S(2)}) copy-start(s32[4096]{0:T(1024)} %param.12) | copy-start | bytes 49156
  7.2 20.0 %copy-start.5 = (s32[8,32]{1,0:T(8,128)S(1)}, s32[8,32]{1,0:T(8,128)}, u32[]{:S(2)}) copy-start(s32[8,32]{1,0:T(8,128)} %param.10) | copy-start | bytes 3076
  9.6 9.5 %all-to-all-start = ((f32[24,4,512]{2,0,1:T(8,128)}), f32[24,4,512]{2,0,1:T(8,128)S(1)}, u32[]{:S(2)}, u32[]{:S(2)}) async-start(f32[24,4,512]{2,0,1:T(8,128)} %pad_maximum_fusion), calls=%async_computation | async-start | bytes 393216 | tf_op jit(solution)/shard_map/all_to_all | solution.py:205
  13.8 83.4 %all-gather.2.cloned.1.call-start = ((), (), s32[]{:S(2)}) async-start(), calls=%async_computation.1 | async-start | bytes 4595712 | tf_op jit(solution)/shard_map/all_gather | solution.py:217
  19.2 0.7 copy-start.1
  74.1 2.5 copy-start.4
  81.0 3.5 %copy-start.2 = (f32[1,8,2048]{2,1,0:T(8,128)S(1)}, f32[1,8,2048]{2,1,0:T(8,128)}, u32[]{:S(2)}) copy-start(f32[1,8,2048]{2,1,0:T(8,128)} %param.8) | copy-start | bytes 196612
  81.0 3.5 %copy-start.3 = (f32[1,8,2048]{2,1,0:T(8,128)S(1)}, f32[1,8,2048]{2,1,0:T(8,128)}, u32[]{:S(2)}) copy-start(f32[1,8,2048]{2,1,0:T(8,128)} %param.7) | copy-start | bytes 196612
Sparse Core Ops, SparseCore 0:
  22.7 63.4 all-gather.1

commit v2 on v1

v2 whole, which is shorter than its diff:
```python
import functools

import jax
import jax.numpy as jnp
from jax import lax
from jax.experimental import pallas as pl
from jax.experimental.pallas import tpu as pltpu
from jax.sharding import PartitionSpec as P

COLORS = 8
SWEEPS = 4
PRIOR_WEIGHT = 1.0
REACH = 2
HIGHEST = lax.Precision.HIGHEST
LANES = 128
EXTRA = 8


def contract_lanes(left, right):
    dims = (((1,), (1,)), ((), ()))
    return lax.dot_general(left, right, dims, precision=HIGHEST, preferred_element_type=jnp.float32)


def couple_kernel(bands, obs, list_len, rows, mix_ref, mix_grid_ref, data_ref, out_ref):
    blocks = data_ref.shape[2] // rows
    full = []
    entry = lax.broadcasted_iota(jnp.int32, (list_len, rows), 0).astype(jnp.float32)
    for block in range(blocks):
        cols = pl.ds(block * rows, rows)
        one_hot, one_hot_mag, star_weight, means = [], [], [], []
        for band in range(bands):
            mags = data_ref[band, 0:obs, cols]
            wts = data_ref[band, obs : 2 * obs, cols]
            slots = data_ref[band, 2 * obs : 3 * obs, cols]
            scaled = wts * mags
            weight_sum = jnp.sum(wts, axis=0, keepdims=True)
            star_weight.append(weight_sum)
            means.append(jnp.sum(scaled, axis=0, keepdims=True) / weight_sum)
            hot = jnp.zeros((list_len, rows), jnp.float32)
            hot_mag = jnp.zeros((list_len, rows), jnp.float32)
            for k in range(obs):
                hit = slots[k : k + 1] == entry
                hot = hot + jnp.where(hit, wts[k : k + 1], 0.0)
                hot_mag = hot_mag + jnp.where(hit, scaled[k : k + 1], 0.0)
            one_hot.append(hot)
            one_hot_mag.append(hot_mag)
        rest = []
        shares = []
        for band in range(bands):
            predicted = mix_ref[band, 0] * means[0]
            for other in range(1, bands):
                predicted = predicted + mix_ref[band, other] * means[other]
            rest.append(one_hot_mag[band] - one_hot[band] * predicted)
            shares.append(one_hot[band] / star_weight[band])
        hot_all = jnp.concatenate(one_hot, axis=0)
        share_all = jnp.concatenate(shares, axis=0)
        rest_all = jnp.concatenate(rest, axis=0)
        coupling = contract_lanes(share_all, hot_all) * mix_grid_ref[...]
        ones = jnp.ones((8, rows), jnp.float32)
        rest_row = contract_lanes(ones, rest_all)
        weight_row = contract_lanes(ones, hot_all)
        first = lax.broadcasted_iota(jnp.int32, (EXTRA, LANES), 0) == 0
        full.append(jnp.concatenate([coupling, jnp.where(first, rest_row, weight_row)], axis=0))
    split = bands // 2
    for part in range(split):
        pieces = []
        for half in range(2):
            band = half * split + part
            for block in range(blocks):
                pieces.append(full[block][:, band * list_len : (band + 1) * list_len])
        out_ref[part] = jnp.concatenate(pieces, axis=1)


def sweep_kernel(bands, list_len, row_count, coupled_ref, pick_ref, color_ref, out_ref, kt, base, tot, rden, zp, stage, sems):
    groups = row_count // 8
    pack = LANES // list_len
    split = bands // 2
    patterns = pick_ref.shape[0]
    depth = stage.shape[0]
    lane = lax.broadcasted_iota(jnp.int32, (8, LANES), 1)
    lane_wide = lax.broadcasted_iota(jnp.int32, (LANES + EXTRA, LANES), 1)

    def fetch(row, slot):
        return pltpu.make_async_copy(
            coupled_ref.at[pl.ds(row * (2 * split), 2 * split)], stage.at[slot], sems.at[slot]
        )

    for row in range(depth - 1):
        fetch(row, row).start()

    def unpack(row, carry):
        slot = lax.rem(row, depth)
        ahead = row + depth - 1

        @pl.when(ahead < row_count)
        def _():
            fetch(ahead, lax.rem(ahead, depth)).start()

        fetch(row, slot).wait()
        group = lax.div(row, 8)
        place = lax.rem(row, 8)
        for part in range(split):
            left = stage[slot, part]
            right = stage[slot, split + part]
            low = jnp.where(lane_wide < LANES // 2, left, pltpu.roll(right, LANES // 2, 1))
            high = jnp.where(lane_wide < LANES // 2, pltpu.roll(left, LANES // 2, 1), right)
            for band, value in ((part, low), (split + part, high)):
                start = (group * bands + band) * (LANES * 8) + place
                kt[pl.ds(start, LANES, stride=8), :] = value[0:LANES]
                base[band, pl.ds(row, 1), :] = value[LANES : LANES + 1]
                tot[band, pl.ds(row + 8, 1), :] = value[LANES + 1 : LANES + 2]
        return carry

    lax.fori_loop(0, row_count, unpack, 0)

    def rows_of(group):
        return pl.ds(pl.multiple_of(group * 8, 8), 8)

    def wrap():
        for band in range(bands):
            tot[band, 0:8, :] = tot[band, row_count : row_count + 8, :]
            tot[band, row_count + 8 : row_count + 16, :] = tot[band, 8:16, :]

    def take(value, picks):
        return jnp.take_along_axis(value, picks, axis=1, mode="promise_in_bounds")

    def gathered(group):
        sums = [jnp.zeros((8, LANES), jnp.float32) for _ in range(2 * bands)]
        for place in range(patterns // pack):
            start = group * 8 + (8 + place - patterns // pack // 2)
            near = [tot[band, pl.ds(start, 8), :] for band in range(bands)]
            for quarter in range(pack):
                pick = pick_ref[place * pack + quarter, rows_of(group), :]
                mask = pick < LANES
                lanes = pick & (LANES - 1)
                for band in range(bands):
                    index = 2 * band + quarter % 2
                    sums[index] = sums[index] + jnp.where(mask, take(near[band], lanes), 0.0)
        return [sums[2 * band] + sums[2 * band + 1] for band in range(bands)]

    def weigh(group, carry):
        for band, value in enumerate(gathered(group)):
            rden[band, rows_of(group), :] = 1.0 / (value + PRIOR_WEIGHT)
        return carry

    wrap()
    lax.fori_loop(0, groups, weigh, 0)
    zp[...] = jnp.zeros_like(zp)

    def step(number, carry):
        color_no = lax.rem(number, COLORS)

        def total(group, inner):
            here = [zp[band, rows_of(group), :] for band in range(bands)]
            sums = [base[band, rows_of(group), :] for band in range(bands)]
            for entry in range(list_len):
                lanes = (lane & (LANES - list_len)) + entry
                values = [take(here[band], lanes) for band in range(bands)]
                for band in range(bands):
                    for other in range(bands):
                        start = (group * bands + band) * (LANES * 8) + (other * list_len + entry) * 8
                        rows = pl.ds(pl.multiple_of(start, 8), 8)
                        sums[band] = sums[band] + values[other] * kt[rows, :]
            for band in range(bands):
                tot[band, pl.ds(pl.multiple_of(group * 8 + 8, 8), 8), :] = sums[band]
            return inner

        lax.fori_loop(0, groups, total, 0, unroll=2)
        wrap()

        def update(group, inner):
            rows = rows_of(group)
            now = color_ref[rows, :] == color_no
            for band, value in enumerate(gathered(group)):
                zp[band, rows, :] = jnp.where(now, value * rden[band, rows, :], zp[band, rows, :])
            return inner

        lax.fori_loop(0, groups, update, 0, unroll=2)

        @pl.when(color_no == COLORS - 1)
        def _():
            out_ref[lax.div(number, COLORS)] = zp[...]

        return carry

    lax.fori_loop(0, SWEEPS * COLORS, step, 0)


def match_kernel(list_len, fields, places, rows_ref, pick_ref):
    pack = LANES // list_len

    def group_picks(group, carry):
        home = rows_ref[pl.ds(pl.multiple_of(group * 8 + 8, 8), 8), :]
        home = jnp.where(home < fields, home, -1)
        near = [rows_ref[pl.ds(group * 8 + 8 + place - places // 2, 8), :] for place in range(places)]
        for quarter in range(pack):
            picks = [jnp.full((8, LANES), LANES, jnp.int32) for _ in range(places)]
            for entry in range(list_len):
                source = quarter * list_len + entry
                for place in range(places):
                    other = jnp.broadcast_to(near[place][:, source : source + 1], (8, LANES))
                    picks[place] = jnp.where(other == home, source, picks[place])
            for place in range(places):
                pick_ref[place * pack + quarter, pl.ds(pl.multiple_of(group * 8, 8), 8), :] = picks[place]
        return carry

    lax.fori_loop(0, pick_ref.shape[1] // 8, group_picks, 0)


def finish_kernel(bands, obs, list_len, rows, mix_ref, data_ref, own_ref, zp_two_ref, zp_own_ref, means_ref, misfit_ref):
    halves = rows // LANES
    pack = LANES // list_len
    mine = data_ref.shape[2] // rows
    first = lax.rem(lax.axis_index("band") * mine, pack)

    def spread(row, picks):
        table = jnp.broadcast_to(row, (obs, LANES))
        return jnp.take_along_axis(table, picks, axis=1, mode="promise_in_bounds")

    for block in range(zp_own_ref.shape[0] * pack):
        row = zp_own_ref[block // pack : block // pack + 1, :]
        for half in range(halves):
            cols = pl.ds(block * rows + half * LANES, LANES)
            wts = own_ref[obs : 2 * obs, cols]
            picks = own_ref[2 * obs : 3 * obs, cols].astype(jnp.int32) + block % pack * list_len
            left = wts * (own_ref[0:obs, cols] - spread(row, picks))
            means_ref[0:1, cols] = jnp.sum(left, axis=0, keepdims=True) / jnp.sum(wts, axis=0, keepdims=True)

    lines = []
    for sweep in range(SWEEPS):
        partial = [jnp.zeros((obs, LANES), jnp.float32) for _ in range(bands)]
        for block in range(mine):
            for half in range(halves):
                cols = pl.ds(block * rows + half * LANES, LANES)
                left, means = [], []
                for band in range(bands):
                    wts = data_ref[band, obs : 2 * obs, cols]
                    picks = data_ref[band, 2 * obs : 3 * obs, cols].astype(jnp.int32) + (first + block) * list_len
                    row = zp_two_ref[sweep, band]
                    mags = data_ref[band, 0:obs, cols] - spread(row, picks)
                    left.append(mags)
                    means.append(jnp.sum(wts * mags, axis=0, keepdims=True) / jnp.sum(wts, axis=0, keepdims=True))
                for band in range(bands):
                    predicted = mix_ref[band, 0] * means[0]
                    for other in range(1, bands):
                        predicted = predicted + mix_ref[band, other] * means[other]
                    wts = data_ref[band, obs : 2 * obs, cols]
                    partial[band] = partial[band] + wts * (left[band] - predicted) ** 2
        lines += [jnp.sum(partial[band], axis=0, keepdims=True) for band in range(bands)]
    block_sums = jnp.concatenate(lines, axis=0)
    misfit_ref[...] = contract_lanes(jnp.ones((8, LANES), jnp.float32), block_sums)[0:1]


def body(magnitudes, weights, slots, block_fields, owner, colors, color_terms):
    bands = color_terms.shape[0]
    tiles = lax.axis_size("sky")
    my_tile = lax.axis_index("sky")
    my_band = lax.axis_index("band")
    _, obs, stars = magnitudes.shape
    blocks, list_len = block_fields.shape
    rows = stars // blocks
    fields = owner.shape[0]
    owned = fields // tiles
    mine = blocks // bands
    pack = LANES // list_len
    tile_rows = blocks // pack
    row_count = tiles * tile_rows
    mixing = (
        jnp.eye(bands, dtype=jnp.float32) + color_terms - jnp.diag(jnp.sum(color_terms, axis=1))
    )
    vmem = pl.BlockSpec(memory_space=pltpu.VMEM)
    smem = pl.BlockSpec(memory_space=pltpu.SMEM)
    hbm = pl.BlockSpec(memory_space=pl.ANY)

    field_no = jnp.arange(fields, dtype=jnp.int32)[:, None]
    flat_fields = block_fields.reshape(1, -1)
    own_colors = jnp.sum(jnp.where(field_no == flat_fields, colors[:, None], 0), axis=0)
    own_colors = jnp.where(flat_fields[0] < fields, own_colors, -1)
    lists = jnp.stack([flat_fields[0], own_colors]).reshape(1, 2, tile_rows, LANES)
    lists = lax.all_gather(lists, "sky", axis=0, tiled=True)
    all_fields = lists[:, 0].reshape(row_count, LANES)
    entry_colors = lists[:, 1].reshape(row_count, LANES)

    own = jnp.concatenate([magnitudes[0], weights[0], slots[0].astype(jnp.float32)], axis=0)
    data = lax.all_to_all(own, "band", split_axis=1, concat_axis=0, tiled=True)
    data = data.reshape(bands, 3 * obs, mine * rows)
    data, all_fields, entry_colors = lax.optimization_barrier((data, all_fields, entry_colors))

    mix_grid = jnp.repeat(jnp.repeat(mixing.T, list_len, axis=0), list_len, axis=1)
    coupled = pl.pallas_call(
        functools.partial(couple_kernel, bands, obs, list_len, rows),
        out_shape=jax.ShapeDtypeStruct((bands // 2, LANES + EXTRA, LANES), jnp.float32),
        in_specs=[smem, vmem, vmem],
        out_specs=vmem,
        name="couple",
    )(mixing, mix_grid, data)
    coupled = lax.all_gather(coupled, ("sky", "band"), axis=0, tiled=True)

    reach_rows = REACH * tile_rows + tile_rows - 1
    padded = jnp.concatenate([all_fields[-8:], all_fields, all_fields[:8]], axis=0)
    places = 2 * reach_rows + 1
    pick = pl.pallas_call(
        functools.partial(match_kernel, list_len, fields, places),
        out_shape=jax.ShapeDtypeStruct((places * pack, row_count, LANES), jnp.int32),
        in_specs=[vmem],
        out_specs=vmem,
        cost_estimate=pl.CostEstimate(flops=10**7, bytes_accessed=10**6, transcendentals=0),
        name="match",
    )(padded)

    big = (bands, row_count, LANES)
    snapshots = pl.pallas_call(
        functools.partial(sweep_kernel, bands, list_len, row_count),
        out_shape=jax.ShapeDtypeStruct((SWEEPS,) + big, jnp.float32),
        in_specs=[hbm, vmem, vmem],
        out_specs=vmem,
        scratch_shapes=[
            pltpu.VMEM((row_count * bands * LANES, LANES), jnp.float32),
            pltpu.VMEM(big, jnp.float32),
            pltpu.VMEM((bands, row_count + 16, LANES), jnp.float32),
            pltpu.VMEM(big, jnp.float32),
            pltpu.VMEM(big, jnp.float32),
            pltpu.VMEM((4, bands, LANES + EXTRA, LANES), jnp.float32),
            pltpu.SemaphoreType.DMA((4,)),
        ],
        compiler_params=pltpu.CompilerParams(vmem_limit_bytes=60 * 1024 * 1024),
        name="sweeps",
    )(coupled, pick, entry_colors)

    final = lax.dynamic_index_in_dim(snapshots[SWEEPS - 1], my_band, 0, keepdims=False)
    zp_tile = lax.dynamic_slice_in_dim(final, my_tile * tile_rows, tile_rows, axis=0)
    my_row = (my_tile * blocks + my_band * mine) // pack
    zp_two = lax.dynamic_slice_in_dim(snapshots, my_row, 1, axis=2)
    star_means, partial = pl.pallas_call(
        functools.partial(finish_kernel, bands, obs, list_len, rows),
        out_shape=(
            jax.ShapeDtypeStruct((1, stars), jnp.float32),
            jax.ShapeDtypeStruct((1, SWEEPS * bands), jnp.float32),
        ),
        in_specs=[smem, vmem, vmem, vmem, vmem],
        out_specs=(vmem, vmem),
        name="finish",
    )(mixing, data, own, zp_two, zp_tile)
    partial = lax.all_gather(partial, ("sky", "band"), axis=0, tiled=True)
    misfit = jnp.sum(partial, axis=0).reshape(SWEEPS, bands) / (obs * stars * tiles)
    misfit = lax.dynamic_slice_in_dim(misfit, my_band, 1, axis=1)

    tile_ids = jnp.mod(my_tile + jnp.arange(3, dtype=jnp.int32) - 1, tiles)

    def close(table):
        by_tile = table.reshape(tiles, tile_rows * LANES)
        parts = [lax.dynamic_index_in_dim(by_tile, tile_ids[n], 0, keepdims=False) for n in range(3)]
        return jnp.concatenate(parts)

    close_fields = close(all_fields)
    is_mine = (owner == my_tile)[:, None]
    rank = jnp.sum((is_mine & (field_no < close_fields[None])).astype(jnp.int32), axis=0)
    has = jnp.sum((is_mine & (field_no == close_fields[None])).astype(jnp.int32), axis=0) > 0
    rank = jnp.where(has, rank, owned)
    entry_no = jnp.arange(close_fields.shape[0], dtype=jnp.int32)[:, None]
    hit = rank[:, None] == jnp.arange(owned, dtype=jnp.int32)[None]
    chosen = jnp.max(jnp.where(hit, entry_no, -1), axis=0)
    own_zp = jnp.sum(jnp.where(chosen[None] == entry_no, close(final)[:, None], 0.0), axis=0)
    return own_zp[None], star_means, misfit


def solution(mesh):
    in_specs = (
        P("band", None, "sky"),
        P("band", None, "sky"),
        P("band", None, "sky"),
        P("sky", None),
        P(),
        P(),
        P(),
    )
    out_specs = (P("band", "sky"), P("band", "sky"), P(None, "band"))
    return jax.shard_map(body, mesh=mesh, in_specs=in_specs, out_specs=out_specs, check_vma=False)
```

time: 264 us -> 210 us (0.80)
  Pallas kernels: 118 us -> 58.3 us
  waiting for transfers between devices: 1.55 us -> 42.2 us
  local copies, waits for them, and re-layouts: 24.6 us -> 7.86 us
  blocking collectives: 70.2 us -> 60.6 us
  other arithmetic: 24.2 us -> 16 us
    pallas_call x1 -> x2, Pallas kernels: 113 us -> 53.5 us  [the longest x1 48.5 us: body(): pl.pallas_call(functools.partial(sweep_kernel, bands, list_len, row_count...]
    all_gather x1, waiting for transfers between devices: 0.01 us -> 42.2 us  [body(): coupled = lax.all_gather(coupled, ('sky', 'band'), axis=0, tiled=True)]
    psum x1 -> x0, blocking collectives: 38.5 us -> none  [body(): misfit = lax.psum(partial, ('sky', 'band')) / (obs * stars * tiles)]
    all_gather x1 -> x2, blocking collectives: 31.7 us -> 60.6 us  [the longest x1 39.1 us: body(): partial = lax.all_gather(partial, ('sky', 'band'), axis=0, tiled=True)]
    select_n x3 -> x1, other arithmetic: 12 us -> 0.01 us  [body(): own_colors = jnp.where(flat_fields[0] < fields, own_colors, -1)]
    gather x2 -> x0, local copies, waits for them, and re-layouts: 11.9 us -> none  [body(): jnp.take(colors, jnp.minimum(all_fields, fields - 1))]
    slice x7 -> x3, local copies, waits for them, and re-layouts: 6.5 us -> 1.18 us  [the longest x1 0.6 us: body(): entry_colors = lists[:, 1].reshape(row_count, LANES)]
  transfers between devices with their start and end apart: 2 -> 2, of which waited for: 1 -> 1; matrix products, arithmetic and copies ran while one was open for 15% -> 8% of each run, Pallas kernels for 0% -> 2%
where the time goes in v2:
time: 210 us; the launch traced here: 209 us
  blocking collectives  60.6 us (29%)
  Pallas kernels  58.3 us (28%)
  waiting for transfers between devices  42.2 us (20%)
  between operations  19.4 us (9%)
  other arithmetic  16 us (8%)
  local copies, waits for them, and re-layouts  7.86 us (4%)
  starting transfers between devices  4.24 us (2%)
    pallas_call x1, Pallas kernels, body(): pl.pallas_call(functools.partial(sweep_kernel, bands, list_len, row_count...  48.5 us
    all_gather x1, waiting for transfers between devices, body(): coupled = lax.all_gather(coupled, ('sky', 'band'), axis=0, tiled=True)  42.2 us
    all_gather x1, blocking collectives, body(): partial = lax.all_gather(partial, ('sky', 'band'), axis=0, tiled=True)  39.1 us
    all_gather x1, blocking collectives, body(): lists = lax.all_gather(lists, 'sky', axis=0, tiled=True)  21.5 us
    pallas_call x1, Pallas kernels, body(): pl.pallas_call(functools.partial(match_kernel, list_len, fields, places),...  4.98 us
    all_to_all x1, starting transfers between devices, body(): data = lax.all_to_all(own, 'band', split_axis=1, concat_axis=0, tiled=True)  4.24 us
  transfers between devices with their start and end apart: 2, of which 1 were waited for; matrix products, arithmetic and copies ran while one was open for 8% of the time, Pallas kernels for 2%

profile of v2, /device:TPU:0, one launch (start us, length us, event | category | flops | bytes accessed | tf_op | source)
XLA Modules:
  0.0 208.6 jit_solution(4851055641553865264)
XLA Ops:
  7.2 0.9 convert_bitcast_fusion
  8.0 1.6 pad_maximum_fusion
  9.6 4.2 %all-to-all-start = ((f32[24,4,512]{2,0,1:T(8,128)}), f32[24,4,512]{2,0,1:T(8,128)S(1)}, u32[]{:S(2)}, u32[]{:S(2)}) async-start(f32[24,4,512]{2,0,1:T(8,128)} %pad_maximum_fusion), calls=%async_computation | async-start | bytes 393216 | tf_op jit(solution)/shard_map/all_to_all | solution.py:285
  13.8 0.8 eq.73
  14.6 0.8 stack.6
  15.3 0.8 reduce_sum.60
  16.1 0.8 fusion.7
  17.0 0.1 reshape.79
  17.1 0.7 copy.24.mix_grid_ref
  17.8 2.5 %select_reduce_fusion = s32[256]{0:T(256)S(1)} fusion(s32[4096]{0:T(1024)} %param.12, s32[256]{0:T(256)S(1)} %eq.73), kind=kLoop, calls=%fused_computation.6 | loop fusion | flops 3145472 | bytes 18432 | tf_op jit(solution)/shard_map/reduce_sum | solution.py:277
  20.3 21.5 %all_gather.9 = s32[8,2,2,128]{3,2,0,1:T(2,128)S(1)} all-gather(s32[1,2,2,128]{3,2,0,1:T(2,128)S(1)} %pad_add_fusion.2), channel_id=1, replica_groups=mesh['sky'=8,'band'=4] {'sky'}, dimensions={0}, use_global_device_ids=true | all-gather | bytes 18432 | tf_op jit(solution)/shard_map/all_gather | solution.py:280
  41.8 0.6 fusion.4
  42.4 1.3 select_subtract_fusion.mix_ref
  43.8 0.7 copy-done
  44.4 2.8 %couple.1 = f32[2,136,128]{2,1,0:T(8,128)} custom-call(f32[4,4]{1,0:T(4,128)} %select_subtract_fusion.mix_ref, f32[128,128]{1,0:T(8,128)} %copy.24.mix_grid_ref, f32[4,24,512]{2,1,0:T(8,128)} %bitcast.34), custom_call_target="tpu_custom_call" | custom-call | tf_op jit(solution)/shard_map/couple/pallas_call | solution.py:290
  47.2 0.6 fusion.6
  53.2 0.7 broadcast_compare_fusion
  53.9 1.6 pad_maximum_fusion.1.own_ref
  55.5 0.6 pad_add_fusion.rows_ref
  56.1 5.0 %match.1.pick_ref = s32[44,16,128]{2,1,0:T(8,128)} custom-call(s32[32,128]{1,0:T(8,128)} %pad_add_fusion.rows_ref), custom_call_target="tpu_custom_call" | custom-call | flops 10000000 | bytes 1000000 | tf_op jit(solution)/shard_map/match/pallas_call | solution.py:302
  61.1 4.1 %convert_reduce_fusion.1 = (s32[768]{0:T(1024)S(1)}, s32[768]{0:T(1024)S(1)}) fusion(s32[768]{0:T(1024)S(1)} %pad_add_fusion.1, pred[4096]{0:T(1024)(128)(4,1)S(1)} %broadcast_compare_fusion), kind=kLoop, calls=%fused_computation.2 | loop fusion | flops 25164288 | bytes 13312 | tf_op jit(solution)/shard_map/reduce_sum | solution.py:358
  65.2 0.3 select_reduce_fusion.2
  65.5 42.2 %all-gather.3.cloned.1.call-done.coupled_ref = f32[64,136,128]{2,1,0:T(8,128)} async-done(((f32[2,136,128]{2,1,0:T(8,128)}), f32[64,136,128]{2,1,0:T(8,128)}) %all-gather.3.cloned.1.call-update) | async-done | bytes 4456464 | tf_op jit(solution)/shard_map/all_gather | solution.py:297
  107.7 48.5 %sweeps.1 = f32[4,4,16,128]{3,2,1,0:T(8,128)} custom-call(f32[64,136,128]{2,1,0:T(8,128)} %all-gather.3.cloned.1.call-done.coupled_ref, s32[44,16,128]{2,1,0:T(8,128)} %match.1.pick_ref, s32[16,128]{1,0:T(8,128)} %bitcast.45), custom_call_target="tpu_custom_call" | custom-call | tf_op jit(solution)/shard_map/sweeps/pallas_call | solution.py:312
  156.2 0.8 slice.37
  156.9 1.4 constant_dynamic-slice_fusion.2.zp_two_ref
  158.4 0.6 fusion.2.zp_own_ref
  159.0 2.0 finish.1
  161.0 39.1 %all-gather = f32[32,1,16]{2,1,0:T(1,128)S(1)} all-gather(f32[1,1,16]{2,1,0:T(1,128)} %bitcast.54), channel_id=1, replica_groups=mesh['sky'=8,'band'=4] {'sky','band'}, dimensions={0}, use_global_device_ids=true | all-gather | bytes 2112 | tf_op jit(solution)/shard_map/all_gather | solution.py:344
  200.1 0.1 div.17
  200.3 0.6 copy.25
  200.9 0.9 select_reduce_fusion.1
  (21 shorter events, 0.3 us)
Async XLA Ops:
  9.6 34.2 %all-to-all-start = ((f32[24,4,512]{2,0,1:T(8,128)}), f32[24,4,512]{2,0,1:T(8,128)S(1)}, u32[]{:S(2)}, u32[]{:S(2)}) async-start(f32[24,4,512]{2,0,1:T(8,128)} %pad_maximum_fusion), calls=%async_computation | async-start | bytes 393216 | tf_op jit(solution)/shard_map/all_to_all | solution.py:285
  13.8 93.8 %all-gather.3.cloned.1.call-start = ((), (), s32[]{:S(2)}) async-start(), calls=%async_computation.1 | async-start | bytes 4595712 | tf_op jit(solution)/shard_map/all_gather | solution.py:297
  43.8 0.7 copy-start
Sparse Core Ops, SparseCore 0:
  47.3 60.2 all-gather.2

commit v3 on v2

--- a/solution.py
+++ b/solution.py
@@ -14,6 +14,7 @@
 HIGHEST = lax.Precision.HIGHEST
 LANES = 128
 EXTRA = 8
+MESH = pl.DeviceIdType.MESH
 
 
 def contract_lanes(left, right):
@@ -186,6 +187,66 @@
     lax.fori_loop(0, SWEEPS * COLORS, step, 0)
 
 
+def greet(axes):
+    barrier = pltpu.get_barrier_semaphore()
+    total = 0
+    for axis, count in axes:
+        for step in range(1, count):
+            peer = lax.rem(lax.axis_index(axis) + step, count)
+            pl.semaphore_signal(barrier, inc=1, device_id={axis: peer}, device_id_type=MESH)
+            total += 1
+    pl.semaphore_wait(barrier, total)
+
+
+def send_all(axis, count, source, target, send_sems, recv_sems, first):
+    me = lax.axis_index(axis)
+    copies = []
+    for step in range(1, count):
+        peer = lax.rem(me + step, count)
+        copy = pltpu.make_async_remote_copy(
+            src_ref=source(peer),
+            dst_ref=target.at[me],
+            send_sem=send_sems.at[first + step - 1],
+            recv_sem=recv_sems.at[first + step - 1],
+            device_id={axis: peer},
+            device_id_type=MESH,
+        )
+        copy.start()
+        copies.append(copy)
+    return copies
+
+
+def exchange_kernel(tiles, bands, lists_ref, own_ref, all_lists_ref, data_ref, send_sems, recv_sems):
+    greet((("sky", tiles), ("band", bands)))
+    copies = send_all("sky", tiles, lambda peer: lists_ref, all_lists_ref, send_sems, recv_sems, 0)
+    copies += send_all("band", bands, lambda peer: own_ref.at[peer], data_ref, send_sems, recv_sems, tiles - 1)
+    my_band = lax.axis_index("band")
+    all_lists_ref[lax.axis_index("sky")] = lists_ref[...]
+    data_ref[my_band] = own_ref[my_band]
+    for copy in copies:
+        copy.wait()
+
+
+def total_kernel(tiles, bands, part_ref, out_ref, by_band, held, by_tile, send_sems, recv_sems):
+    greet((("sky", tiles), ("band", bands)))
+    copies = send_all("band", bands, lambda peer: part_ref, by_band, send_sems, recv_sems, tiles - 1)
+    by_band[lax.axis_index("band")] = part_ref[...]
+    for copy in copies:
+        copy.wait()
+    total = by_band[0]
+    for band in range(1, bands):
+        total = total + by_band[band]
+    held[...] = total
+    copies = send_all("sky", tiles, lambda peer: held, by_tile, send_sems, recv_sems, 0)
+    by_tile[lax.axis_index("sky")] = total
+    for copy in copies:
+        copy.wait()
+    total = by_tile[0]
+    for tile in range(1, tiles):
+        total = total + by_tile[tile]
+    out_ref[...] = total
+
+
 def match_kernel(list_len, fields, places, rows_ref, pick_ref):
     pack = LANES // list_len
 
@@ -247,8 +308,9 @@
                     wts = data_ref[band, obs : 2 * obs, cols]
                     partial[band] = partial[band] + wts * (left[band] - predicted) ** 2
         lines += [jnp.sum(partial[band], axis=0, keepdims=True) for band in range(bands)]
+    lines.append(jnp.zeros((LANES - len(lines), LANES), jnp.float32))
     block_sums = jnp.concatenate(lines, axis=0)
-    misfit_ref[...] = contract_lanes(jnp.ones((8, LANES), jnp.float32), block_sums)[0:1]
+    misfit_ref[...] = contract_lanes(jnp.ones((8, LANES), jnp.float32), block_sums)
 
 
 def body(magnitudes, weights, slots, block_fields, owner, colors, color_terms):
@@ -276,15 +338,25 @@
     flat_fields = block_fields.reshape(1, -1)
     own_colors = jnp.sum(jnp.where(field_no == flat_fields, colors[:, None], 0), axis=0)
     own_colors = jnp.where(flat_fields[0] < fields, own_colors, -1)
-    lists = jnp.stack([flat_fields[0], own_colors]).reshape(1, 2, tile_rows, LANES)
-    lists = lax.all_gather(lists, "sky", axis=0, tiled=True)
+    lists = jnp.stack([flat_fields[0], own_colors]).reshape(2 * tile_rows, LANES)
+    own = jnp.concatenate([magnitudes[0], weights[0], slots[0].astype(jnp.float32)], axis=0)
+    by_peer = own.reshape(3 * obs, bands, mine * rows).transpose(1, 0, 2)
+    peers = tiles + bands - 2
+    lists, data = pl.pallas_call(
+        functools.partial(exchange_kernel, tiles, bands),
+        out_shape=(
+            jax.ShapeDtypeStruct((tiles,) + lists.shape, jnp.int32),
+            jax.ShapeDtypeStruct(by_peer.shape, jnp.float32),
+        ),
+        in_specs=[vmem, vmem],
+        out_specs=(vmem, vmem),
+        scratch_shapes=[pltpu.SemaphoreType.DMA((peers,)), pltpu.SemaphoreType.DMA((peers,))],
+        compiler_params=pltpu.CompilerParams(collective_id=0, has_side_effects=True),
+        name="exchange",
+    )(lists, by_peer)
+    lists = lists.reshape(tiles, 2, tile_rows, LANES)
     all_fields = lists[:, 0].reshape(row_count, LANES)
     entry_colors = lists[:, 1].reshape(row_count, LANES)
-
-    own = jnp.concatenate([magnitudes[0], weights[0], slots[0].astype(jnp.float32)], axis=0)
-    data = lax.all_to_all(own, "band", split_axis=1, concat_axis=0, tiled=True)
-    data = data.reshape(bands, 3 * obs, mine * rows)
-    data, all_fields, entry_colors = lax.optimization_barrier((data, all_fields, entry_colors))
 
     mix_grid = jnp.repeat(jnp.repeat(mixing.T, list_len, axis=0), list_len, axis=1)
     coupled = pl.pallas_call(
@@ -335,14 +407,29 @@
         functools.partial(finish_kernel, bands, obs, list_len, rows),
         out_shape=(
             jax.ShapeDtypeStruct((1, stars), jnp.float32),
-            jax.ShapeDtypeStruct((1, SWEEPS * bands), jnp.float32),
+            jax.ShapeDtypeStruct((8, LANES), jnp.float32),
         ),
         in_specs=[smem, vmem, vmem, vmem, vmem],
         out_specs=(vmem, vmem),
         name="finish",
     )(mixing, data, own, zp_two, zp_tile)
-    partial = lax.all_gather(partial, ("sky", "band"), axis=0, tiled=True)
-    misfit = jnp.sum(partial, axis=0).reshape(SWEEPS, bands) / (obs * stars * tiles)
+    slab = (8, LANES)
+    total = pl.pallas_call(
+        functools.partial(total_kernel, tiles, bands),
+        out_shape=jax.ShapeDtypeStruct(slab, jnp.float32),
+        in_specs=[vmem],
+        out_specs=vmem,
+        scratch_shapes=[
+            pltpu.VMEM((bands,) + slab, jnp.float32),
+            pltpu.VMEM(slab, jnp.float32),
+            pltpu.VMEM((tiles,) + slab, jnp.float32),
+            pltpu.SemaphoreType.DMA((peers,)),
+            pltpu.SemaphoreType.DMA((peers,)),
+        ],
+        compiler_params=pltpu.CompilerParams(collective_id=1, has_side_effects=True),
+        name="total",
+    )(partial)
+    misfit = total[0, : SWEEPS * bands].reshape(SWEEPS, bands) / (obs * stars * tiles)
     misfit = lax.dynamic_slice_in_dim(misfit, my_band, 1, axis=1)
 
     tile_ids = jnp.mod(my_tile + jnp.arange(3, dtype=jnp.int32) - 1, tiles)

time: 210 us -> 169 us (0.80)
  blocking collectives: 60.6 us -> 0 us
  Pallas kernels: 58.3 us -> 80.5 us
  starting transfers between devices: 4.24 us -> 0.04 us
    all_gather x2 -> x0, blocking collectives: 60.6 us -> none  [the longest x1 39.1 us: body(): partial = lax.all_gather(partial, ('sky', 'band'), axis=0, tiled=True)]
    pallas_call x0 -> x2, Pallas kernels: none -> 22.2 us  [the longest x1 11.4 us: body(): pl.pallas_call(functools.partial(exchange_kernel, tiles, bands), out_shap...]
    all_to_all x1 -> x0, starting transfers between devices: 4.24 us -> none  [body(): data = lax.all_to_all(own, 'band', split_axis=1, concat_axis=0, tiled=True)]
  transfers between devices with their start and end apart: 2 -> 1, of which waited for: 1 -> 1; matrix products, arithmetic and copies ran while one was open for 8% -> 6% of each run, Pallas kernels for 2% -> 3%
where the time goes in v3:
time: 169 us; the launch traced here: 168 us
  Pallas kernels  80.5 us (48%)
  waiting for transfers between devices  42 us (25%)
  between operations  19.5 us (12%)
  other arithmetic  16.6 us (10%)
  local copies, waits for them, and re-layouts  9.16 us (5%)
    pallas_call x1, Pallas kernels, body(): pl.pallas_call(functools.partial(sweep_kernel, bands, list_len, row_count...  48.5 us
    all_gather x1, waiting for transfers between devices, body(): coupled = lax.all_gather(coupled, ('sky', 'band'), axis=0, tiled=True)  42 us
    pallas_call x1, Pallas kernels, body(): pl.pallas_call(functools.partial(exchange_kernel, tiles, bands), out_shap...  11.4 us
    pallas_call x1, Pallas kernels, body(): pl.pallas_call(functools.partial(total_kernel, tiles, bands), out_shape=j...  10.8 us
    pallas_call x1, Pallas kernels, body(): pl.pallas_call(functools.partial(match_kernel, list_len, fields, places),...  4.98 us
    reduce_sum x1, other arithmetic, body(): jnp.sum((is_mine & (field_no == close_fields[None])).astype(jnp.int32), a...  4.05 us
  transfers between devices with their start and end apart: 1, of which 1 were waited for; matrix products, arithmetic and copies ran while one was open for 6% of the time, Pallas kernels for 3%

profile of v3, /device:TPU:0, one launch (start us, length us, event | category | flops | bytes accessed | tf_op | source)
XLA Modules:
  0.0 167.8 jit_solution(6352156396922890970)
XLA Ops:
  7.2 0.8 reduce_sum.51
  8.0 1.3 select_subtract_fusion.mix_ref
  9.3 0.8 fusion.6
  10.1 0.8 eq.73
  10.9 0.8 stack_squeeze_reshape.3
  11.7 0.1 reshape.71
  11.8 0.7 copy.29.mix_grid_ref
  12.5 2.5 %select_reduce_fusion = s32[256]{0:T(256)S(1)} fusion(s32[4096]{0:T(1024)} %param.12, s32[256]{0:T(256)S(1)} %eq.73), kind=kLoop, calls=%fused_computation.6 | loop fusion | flops 3145472 | bytes 18432 | tf_op jit(solution)/shard_map/reduce_sum | solution.py:339
  15.0 0.6 reshape.69.lists_ref
  15.6 0.8 convert_bitcast_fusion
  16.4 1.6 maximum_bitcast_fusion.own_ref
  18.0 11.4 %exchange.1 = (s32[8,4,128]{2,1,0:T(4,128)}, f32[4,24,512]{2,1,0:T(8,128)}) custom-call(s32[4,128]{1,0:T(4,128)} %reshape.69.lists_ref, f32[4,24,512]{2,1,0:T(8,128)} %maximum_bitcast_fusion.own_ref), custom_call_target="tpu_custom_call" | custom-call | tf_op jit(solution)/shard_map/exchange/pallas_call | solution.py:345
  29.4 2.8 %couple.1 = f32[2,136,128]{2,1,0:T(8,128)} custom-call(f32[4,4]{1,0:T(4,128)} %select_subtract_fusion.mix_ref, f32[128,128]{1,0:T(8,128)} %copy.29.mix_grid_ref, f32[4,24,512]{2,1,0:T(8,128)} %get-tuple-element.8.data_ref), custom_call_target="tpu_custom_call" | custom-call | tf_op jit(solution)/shard_map/couple/pallas_call | solution.py:362
  32.2 0.6 fusion.5
  36.4 1.3 slice_bitcast_fusion
  39.5 0.7 fusion.4
  40.2 0.6 pad_add_fusion.rows_ref
  40.8 5.0 %match.1.pick_ref = s32[44,16,128]{2,1,0:T(8,128)} custom-call(s32[32,128]{1,0:T(8,128)} %pad_add_fusion.rows_ref), custom_call_target="tpu_custom_call" | custom-call | flops 10000000 | bytes 1000000 | tf_op jit(solution)/shard_map/match/pallas_call | solution.py:374
  45.8 0.7 broadcast_compare_fusion
  46.5 4.1 %convert_reduce_fusion.1 = (s32[768]{0:T(1024)S(1)}, s32[768]{0:T(1024)S(1)}) fusion(s32[768]{0:T(1024)S(1)} %pad_add_fusion.1, pred[4096]{0:T(1024)(128)(4,1)S(1)} %broadcast_compare_fusion), kind=kLoop, calls=%fused_computation.2 | loop fusion | flops 25164288 | bytes 13312 | tf_op jit(solution)/shard_map/reduce_sum | solution.py:445
  50.6 0.3 select_reduce_fusion.2
  50.9 1.6 pad_maximum_fusion.own_ref
  52.5 42.0 %all-gather.2.cloned.1.call-done.coupled_ref = f32[64,136,128]{2,1,0:T(8,128)} async-done(((f32[2,136,128]{2,1,0:T(8,128)}), f32[64,136,128]{2,1,0:T(8,128)}) %all-gather.2.cloned.1.call-update) | async-done | bytes 4456464 | tf_op jit(solution)/shard_map/all_gather | solution.py:369
  94.5 48.5 %sweeps.1 = f32[4,4,16,128]{3,2,1,0:T(8,128)} custom-call(f32[64,136,128]{2,1,0:T(8,128)} %all-gather.2.cloned.1.call-done.coupled_ref, s32[44,16,128]{2,1,0:T(8,128)} %match.1.pick_ref, s32[16,128]{1,0:T(8,128)} %bitcast.57), custom_call_target="tpu_custom_call" | custom-call | tf_op jit(solution)/shard_map/sweeps/pallas_call | solution.py:384
  143.0 0.8 slice.53
  143.8 1.4 constant_dynamic-slice_fusion.2.zp_two_ref
  145.2 0.6 fusion.2.zp_own_ref
  145.8 2.0 %finish.1 = (f32[1,2048]{1,0:T(1,128)}, f32[8,128]{1,0:T(8,128)}) custom-call(f32[4,4]{1,0:T(4,128)} %select_subtract_fusion.mix_ref, f32[4,24,512]{2,1,0:T(8,128)} %get-tuple-element.8.data_ref, f32[24,2048]{1,0:T(8,128)} %pad_maximum_fusion.own_ref, f32[4,4,1,128]{3,2,1,0:T(1,128)} %constant_dynamic-slice_fusion.2.zp_two_ref, f32[2,128]{1,0:T(2,128)} %fusion.2.zp_own_ref), custom_call_target="tpu_custom_call" | custom-call | tf_op jit(solution)/shard_map/finish/pallas_call | solution.py:406
  147.8 10.8 %total.1 = f32[8,128]{1,0:T(8,128)} custom-call(f32[8,128]{1,0:T(8,128)} %get-tuple-element.10.part_ref), custom_call_target="tpu_custom_call" | custom-call | tf_op jit(solution)/shard_map/total/pallas_call | solution.py:417
  158.6 0.7 multiply_reduce_fusion
  159.5 0.6 copy.33
  160.1 0.9 select_reduce_fusion.1
  (17 shorter events, 0.4 us)
Async XLA Ops:
  7.2 87.3 %all-gather.2.cloned.1.call-start = ((), (), s32[]{:S(2)}) async-start(), calls=%async_computation | async-start | bytes 4595712 | tf_op jit(solution)/shard_map/all_gather | solution.py:369
Sparse Core Ops, SparseCore 0:
  32.3 62.0 all-gather.1

commit v4 on v3

--- a/solution.py
+++ b/solution.py
@@ -227,6 +227,62 @@
         copy.wait()
 
 
+def spread_kernel(high_count, own_ref, all_ref, send_sems, recv_sems):
+    sky, band = lax.axis_index("sky"), lax.axis_index("band")
+    high, low = sky // 2, sky % 2
+    side, core = band // 2, band % 2
+    highs = [lax.rem(high + step, high_count) for step in range(1, high_count)]
+    to_low = {"sky": high * 2 + (1 - low)}
+    to_side = {"band": (1 - side) * 2 + core}
+    to_core = {"band": side * 2 + (1 - core)}
+    peers = [{"sky": peer * 2 + low} for peer in highs] + [to_low, to_side, to_core]
+    barrier = pltpu.get_barrier_semaphore()
+    for peer in peers:
+        pl.semaphore_signal(barrier, inc=1, device_id=peer, device_id_type=MESH)
+    pl.semaphore_wait(barrier, len(peers))
+    count = [0]
+
+    def send(source, target, peer):
+        copy = pltpu.make_async_remote_copy(
+            src_ref=source,
+            dst_ref=target,
+            send_sem=send_sems.at[count[0]],
+            recv_sem=recv_sems.at[count[0]],
+            device_id=peer,
+            device_id_type=MESH,
+        )
+        count[0] += 1
+        copy.start()
+        return copy
+
+    def wait(copies):
+        for copy in copies:
+            copy.wait()
+
+    mine = all_ref.at[high, low, side, core]
+    copies = [send(own_ref, mine, peer) for peer in peers[: high_count - 1]]
+    all_ref[high, low, side, core] = own_ref[...]
+    wait(copies)
+
+    column = all_ref.at[:, low, side, core]
+    first = all_ref.at[:, low, side, core, 0]
+    second = all_ref.at[:, low, side, core, 1]
+    copies = [send(first, first, to_low), send(second, second, to_side)]
+    late = [send(column, column, to_core)]
+    wait(copies)
+
+    first = all_ref.at[:, :, side, core, 0]
+    second = all_ref.at[:, low, :, core, 1]
+    copies = [send(first, first, to_side), send(second, second, to_low)]
+    for part in (all_ref.at[:, 1 - low, side, core, 0], all_ref.at[:, low, 1 - side, core, 1]):
+        late.append(send(part, part, to_core))
+    wait(copies)
+
+    for part in (all_ref.at[:, :, 1 - side, core, 0], all_ref.at[:, 1 - low, :, core, 1]):
+        late.append(send(part, part, to_core))
+    wait(late)
+
+
 def total_kernel(tiles, bands, part_ref, out_ref, by_band, held, by_tile, send_sems, recv_sems):
     greet((("sky", tiles), ("band", bands)))
     copies = send_all("band", bands, lambda peer: part_ref, by_band, send_sems, recv_sems, tiles - 1)
@@ -366,7 +422,20 @@
         out_specs=vmem,
         name="couple",
     )(mixing, mix_grid, data)
-    coupled = lax.all_gather(coupled, ("sky", "band"), axis=0, tiled=True)
+    everyone = (tiles // 2, 2, bands // 2, 2) + coupled.shape
+    copies = tiles // 2 - 1 + 9
+    coupled = pl.pallas_call(
+        functools.partial(spread_kernel, tiles // 2),
+        out_shape=jax.ShapeDtypeStruct(everyone, jnp.float32),
+        in_specs=[vmem],
+        out_specs=vmem,
+        scratch_shapes=[pltpu.SemaphoreType.DMA((copies,)), pltpu.SemaphoreType.DMA((copies,))],
+        compiler_params=pltpu.CompilerParams(
+            collective_id=2, has_side_effects=True, vmem_limit_bytes=60 * 1024 * 1024
+        ),
+        name="spread",
+    )(coupled)
+    coupled = coupled.reshape((-1,) + coupled.shape[-2:])
 
     reach_rows = REACH * tile_rows + tile_rows - 1
     padded = jnp.concatenate([all_fields[-8:], all_fields, all_fields[:8]], axis=0)

time: 169 us -> 150 us (0.89)
  waiting for transfers between devices: 42 us -> 0 us
  Pallas kernels: 80.5 us -> 120 us
  between operations: 19.5 us -> 6.62 us
    all_gather x1 -> x0, waiting for transfers between devices: 42 us -> none  [body(): coupled = lax.all_gather(coupled, ('sky', 'band'), axis=0, tiled=True)]
    pallas_call x0 -> x1, Pallas kernels: none -> 37.8 us  [body(): pl.pallas_call(functools.partial(spread_kernel, tiles // 2), out_shape=ja...]
    pallas_call x1, Pallas kernels: 10.8 us -> 12.6 us  [body(): pl.pallas_call(functools.partial(total_kernel, tiles, bands), out_shape=j...]
  transfers between devices with their start and end apart: 1 -> 0, of which waited for: 1 -> 0; matrix products, arithmetic and copies ran while one was open for 6% -> 0% of each run, Pallas kernels for 3% -> 0%
where the time goes in v4:
time: 150 us; the launch traced here: 149 us
  Pallas kernels  120 us (80%)
  other arithmetic  15.1 us (10%)
  local copies, waits for them, and re-layouts  7.76 us (5%)
  between operations  6.62 us (4%)
    pallas_call x1, Pallas kernels, body(): pl.pallas_call(functools.partial(sweep_kernel, bands, list_len, row_count...  48.5 us
    pallas_call x1, Pallas kernels, body(): pl.pallas_call(functools.partial(spread_kernel, tiles // 2), out_shape=ja...  37.8 us
    pallas_call x1, Pallas kernels, body(): pl.pallas_call(functools.partial(total_kernel, tiles, bands), out_shape=j...  12.6 us
    pallas_call x1, Pallas kernels, body(): pl.pallas_call(functools.partial(exchange_kernel, tiles, bands), out_shap...  11.4 us
    pallas_call x1, Pallas kernels, body(): pl.pallas_call(functools.partial(match_kernel, list_len, fields, places),...  4.98 us
    reduce_sum x1, other arithmetic, body(): jnp.sum((is_mine & (field_no == close_fields[None])).astype(jnp.int32), a...  4.08 us

profile of v4, /device:TPU:0, one launch (start us, length us, event | category | flops | bytes accessed | tf_op | source)
XLA Modules:
  0.0 149.5 jit_solution(14357543811500834752)
XLA Ops:
  0.6 0.8 reduce_sum.51
  1.4 1.3 select_subtract_fusion.mix_ref
  2.8 0.8 fusion.6
  3.6 0.1 reshape.74
  3.7 0.7 copy.23.mix_grid_ref
  4.4 0.8 eq.73
  5.2 2.5 %select_reduce_fusion = s32[256]{0:T(256)S(1)} fusion(s32[4096]{0:T(1024)} %param.12, s32[256]{0:T(256)S(1)} %eq.73), kind=kLoop, calls=%fused_computation.6 | loop fusion | flops 3145472 | bytes 18432 | tf_op jit(solution)/shard_map/reduce_sum | solution.py:395
  7.7 0.8 stack_squeeze_reshape.3
  8.4 0.6 reshape.72.lists_ref
  9.0 0.8 convert_bitcast_fusion
  9.9 1.6 %maximum_bitcast_fusion.own_ref = f32[4,24,512]{2,1,0:T(8,128)} fusion(f32[8,4,512]{2,0,1:T(8,128)S(1)} %bitcast.51, f32[8,4,512]{2,0,1:T(8,128)} %bitcast.53, f32[8,4,512]{2,0,1:T(8,128)} %bitcast.55), kind=kLoop, calls=%fused_computation.12 | loop fusion | flops 98304 | bytes 393216 | tf_op jit(solution)/shard_map/transpose | solution.py:399
  11.4 11.4 %exchange.1 = (s32[8,4,128]{2,1,0:T(4,128)}, f32[4,24,512]{2,1,0:T(8,128)}) custom-call(s32[4,128]{1,0:T(4,128)} %reshape.72.lists_ref, f32[4,24,512]{2,1,0:T(8,128)} %maximum_bitcast_fusion.own_ref), custom_call_target="tpu_custom_call" | custom-call | tf_op jit(solution)/shard_map/exchange/pallas_call | solution.py:401
  22.9 2.8 %couple.1.own_ref = f32[2,136,128]{2,1,0:T(8,128)} custom-call(f32[4,4]{1,0:T(4,128)} %select_subtract_fusion.mix_ref, f32[128,128]{1,0:T(8,128)} %copy.23.mix_grid_ref, f32[4,24,512]{2,1,0:T(8,128)} %get-tuple-element.8.data_ref), custom_call_target="tpu_custom_call" | custom-call | tf_op jit(solution)/shard_map/couple/pallas_call | solution.py:418
  25.6 37.8 %spread.1 = f32[4,2,2,2,2,136,128]{6,5,4,3,2,1,0:T(8,128)} custom-call(f32[2,136,128]{2,1,0:T(8,128)} %couple.1.own_ref), custom_call_target="tpu_custom_call" | custom-call | tf_op jit(solution)/shard_map/spread/pallas_call | solution.py:427
  63.4 0.6 slice_bitcast_fusion
  64.1 0.6 pad_add_fusion.rows_ref
  64.7 5.0 %match.1.pick_ref = s32[44,16,128]{2,1,0:T(8,128)} custom-call(s32[32,128]{1,0:T(8,128)} %pad_add_fusion.rows_ref), custom_call_target="tpu_custom_call" | custom-call | flops 10000000 | bytes 1000000 | tf_op jit(solution)/shard_map/match/pallas_call | solution.py:443
  69.6 48.5 %sweeps.1 = f32[4,4,16,128]{3,2,1,0:T(8,128)} custom-call(f32[64,136,128]{2,1,0:T(8,128)} %bitcast.50, s32[44,16,128]{2,1,0:T(8,128)} %match.1.pick_ref, s32[16,128]{1,0:T(8,128)} %bitcast.59), custom_call_target="tpu_custom_call" | custom-call | tf_op jit(solution)/shard_map/sweeps/pallas_call | solution.py:453
  118.1 0.8 slice.53
  118.9 0.6 fusion.5
  125.4 4.1 %convert_reduce_fusion.1 = (s32[768]{0:T(1024)S(1)}, s32[768]{0:T(1024)S(1)}) fusion(s32[768]{0:T(1024)S(1)} %pad_add_fusion.1, pred[4096]{0:T(1024)(128)(4,1)S(1)} %broadcast_compare_fusion), kind=kLoop, calls=%fused_computation.2 | loop fusion | flops 25164288 | bytes 13312 | tf_op jit(solution)/shard_map/reduce_sum | solution.py:514
  129.5 0.3 select_reduce_fusion.2
  129.8 0.9 select_reduce_fusion.1
  130.7 0.7 pad_maximum_fusion.own_ref
  131.4 1.4 constant_dynamic-slice_fusion.2.zp_two_ref
  132.8 0.5 fusion.2.zp_own_ref
  133.3 2.0 %finish.1 = (f32[1,2048]{1,0:T(1,128)}, f32[8,128]{1,0:T(8,128)}) custom-call(f32[4,4]{1,0:T(4,128)} %select_subtract_fusion.mix_ref, f32[4,24,512]{2,1,0:T(8,128)} %get-tuple-element.8.data_ref, f32[24,2048]{1,0:T(8,128)} %pad_maximum_fusion.own_ref, f32[4,4,1,128]{3,2,1,0:T(1,128)} %constant_dynamic-slice_fusion.2.zp_two_ref, f32[2,128]{1,0:T(2,128)} %fusion.2.zp_own_ref), custom_call_target="tpu_custom_call" | custom-call | tf_op jit(solution)/shard_map/finish/pallas_call | solution.py:475
  135.4 12.6 %total.1 = f32[8,128]{1,0:T(8,128)} custom-call(f32[8,128]{1,0:T(8,128)} %get-tuple-element.10.part_ref), custom_call_target="tpu_custom_call" | custom-call | tf_op jit(solution)/shard_map/total/pallas_call | solution.py:486
  148.0 0.7 multiply_reduce_fusion
  148.7 0.1 div.17
  148.8 0.1 constant_dynamic-slice_fusion
  148.9 0.6 copy.27
  (23 shorter events, 0.2 us)
Async XLA Ops:
  22.9 40.6 %copy-start.2 = (s32[8,4,128]{2,1,0:T(4,128)S(1)}, s32[8,4,128]{2,1,0:T(4,128)}, u32[]{:S(2)}) copy-start(s32[8,4,128]{2,1,0:T(4,128)} %get-tuple-element.7) | copy-start | bytes 49156
  63.4 62.0 %copy-start.3 = (s32[4096]{0:T(1024)S(1)}, s32[4096]{0:T(1024)}, u32[]{:S(2)}) copy-start(s32[4096]{0:T(1024)} %param.11) | copy-start | bytes 49156
  63.4 67.3 %copy-start = (f32[1,8,2048]{2,1,0:T(8,128)S(1)}, f32[1,8,2048]{2,1,0:T(8,128)}, u32[]{:S(2)}) copy-start(f32[1,8,2048]{2,1,0:T(8,128)} %param.8) | copy-start | bytes 196612
  63.4 67.3 %copy-start.1 = (f32[1,8,2048]{2,1,0:T(8,128)S(1)}, f32[1,8,2048]{2,1,0:T(8,128)}, u32[]{:S(2)}) copy-start(f32[1,8,2048]{2,1,0:T(8,128)} %param.7) | copy-start | bytes 196612
